TPU v7x, 32 devices: a whole 2x2x4 slice. The times are simulated.
32 devices in a mesh: grp: 4 (over y, x), dev: 8 (over z, core).
Axes of the slice: x: 2, y: 2, z: 4, core: 2. Of those that a mesh axis runs over, the one named last changes fastest.
Arguments:
- table: bfloat16 [8, 32768, 256], P('grp', 'dev'), may hold values from -0.75 to 0.75
- token_ids: int32 [8192], P(('grp', 'dev')), may hold values from 0 to 32767, as said below
- hidden: bfloat16 [8192, 2560], P(('grp', 'dev')), may hold values from -6 to 6
- w_proj: bfloat16 [2560, 2048], replicated, may hold values from -0.125 to 0.125
- norm_gain: float32 [256], replicated, may hold values from 0.5 to 1.5
Outputs:
- served_table: bfloat16 [8, 4, 1024, 2048], P('dev', 'grp')
- layer_inputs: bfloat16 [8192, 8, 256], P(('grp', 'dev'))
Inputs may be any that keep to these rules, and one draw needn't show every extreme that they name: `token_ids`: of the 256 tokens of one device, at most 16 have ids in any one aligned block of 1024 vocabulary rows, and exactly 16 in some block.
All inputs are finite; a program needn't handle non-finite values.
Results may differ from a plain program's by a relative error of at most 0.001.
Values may be sent and summed in bfloat16 or wider, within the bound.
A program may use at most 128 MiB of HBM per device.

v0:
```python
import math

import jax
import jax.numpy as jnp
from jax import lax
from jax.sharding import PartitionSpec as P


def lookup(all_ids, local_rows, base):
    owned = local_rows.shape[0]
    count = all_ids.shape[0]
    block = math.gcd(count, 512)
    blocks = all_ids.reshape(count // block, block)

    def one_block(ids_block):
        onehot = (ids_block[:, None] - base == jnp.arange(owned, dtype=jnp.int32)[None, :]).astype(
            jnp.bfloat16
        )
        return jnp.dot(onehot, local_rows, preferred_element_type=jnp.float32).astype(jnp.bfloat16)

    return lax.map(one_block, blocks).reshape(count, local_rows.shape[1])


def on_device(table, token_ids, hidden, w_proj, norm_gain):
    n_grp = lax.axis_size("grp")
    n_dev = lax.axis_size("dev")
    g_index = lax.axis_index("grp")
    d_index = lax.axis_index("dev")
    layer_share, vocab_share, width = table.shape
    layers = layer_share * n_grp
    tok_count = token_ids.shape[0]
    moved = lax.all_to_all(table, "grp", split_axis=1, concat_axis=0, tiled=True)
    row_count = moved.shape[1]
    served_rows = jnp.transpose(moved, (1, 0, 2)).reshape(row_count, layers * width)
    served_table = served_rows.reshape(1, 1, row_count, layers * width)
    peers = n_grp * n_dev
    capacity = max(2, 2 * tok_count // peers)
    owner_block = token_ids // row_count
    owner_peer = owner_block % n_grp * n_dev + owner_block // n_grp
    positions = jnp.arange(tok_count, dtype=jnp.int32)
    same_peer = owner_peer[:, None] == owner_peer[None, :]
    earlier = positions[None, :] < positions[:, None]
    slot_index = jnp.sum((same_peer & earlier).astype(jnp.int32), axis=1)
    wanted = owner_peer * capacity + slot_index
    slot_hit = (wanted[:, None] == jnp.arange(peers * capacity, dtype=jnp.int32)[None, :]).astype(
        jnp.int32
    )
    outgoing = jnp.sum(slot_hit * (token_ids + 1)[:, None], axis=0) - 1
    base = (d_index * n_grp + g_index) * row_count
    incoming = lax.all_to_all(
        outgoing.reshape(peers, capacity), ("grp", "dev"), split_axis=0, concat_axis=0, tiled=True
    )
    found = lookup(incoming.reshape(peers * capacity), served_rows, base)
    found = found.reshape(peers, capacity, layers * width)
    replies = lax.all_to_all(found, ("grp", "dev"), split_axis=0, concat_axis=0, tiled=True)
    picker = slot_hit.astype(jnp.bfloat16)
    emb = jnp.dot(
        picker,
        replies.reshape(peers * capacity, layers * width),
        preferred_element_type=jnp.float32,
    )
    proj = jnp.dot(hidden, w_proj, preferred_element_type=jnp.float32).reshape(
        tok_count, layers, width
    )
    mean_sq = jnp.mean(proj * proj, axis=-1, keepdims=True)
    normed = proj / jnp.sqrt(mean_sq + 1e-06) * norm_gain
    emb = emb.reshape(tok_count, layers, width)
    layer_inputs = ((normed + math.sqrt(width) * emb) / math.sqrt(2.0)).astype(jnp.bfloat16)
    return (served_table, layer_inputs)


def solution(mesh):
    in_specs = (P("grp", "dev", None), P(("grp", "dev")), P(("grp", "dev"), None), P(), P())
    out_specs = (P("dev", "grp", None, None), P(("grp", "dev"), None, None))
    return jax.shard_map(
        on_device, mesh=mesh, in_specs=in_specs, out_specs=out_specs, check_vma=False
    )
```

profile of v0, /device:TPU:0, one launch (start us, length us, event | category | flops | bytes accessed | tf_op | source)
XLA Modules:
  0.0 152.2 jit_solution(1475072987152448503)
XLA Ops:
  0.6 0.0 copy-start
  0.6 0.8 fusion.10
  1.4 0.2 convert_reduce_fusion
  1.6 0.2 select_reduce_fusion
  1.8 0.7 sub.35
  2.5 7.3 %all-to-all-start.1 = ((s32[32,1,16]{2,1,0:T(1,128)}), s32[32,1,16]{2,1,0:T(1,128)S(1)}, u32[]{:S(2)}, u32[]{:S(2)}) async-start(s32[32,1,16]{2,1,0:T(1,128)} %bitcast.6), calls=%async_computation.1 | async-start | bytes 32768 | tf_op jit(solution)/shard_map/all_to_all | solution.py:50
  9.8 10.1 %copy.49 = bf16[2,4096,256]{2,0,1:T(2,128)(2,1)} copy(bf16[2,4096,256]{2,1,0:T(8,128)(2,1)} %param.5) | data formatting | bytes 8388608 | tf_op args[0]
  19.9 0.0 all-to-all-done.1
  19.9 4.9 %all-to-all-start = ((bf16[2,4096,256]{2,0,1:T(2,128)(2,1)}), bf16[2,4096,256]{2,0,1:T(2,128)(2,1)}, u32[]{:S(2)}, u32[]{:S(2)}) async-start(bf16[2,4096,256]{2,0,1:T(2,128)(2,1)} %copy.49), calls=%async_computation | async-start | bytes 8388608 | tf_op jit(solution)/shard_map/all_to_all | solution.py:32
  24.9 0.1 sub.38
  24.9 48.0 %all-to-all-done = bf16[2,4096,256]{2,0,1:T(2,128)(2,1)} async-done(((bf16[2,4096,256]{2,0,1:T(2,128)(2,1)}), bf16[2,4096,256]{2,0,1:T(2,128)(2,1)}, u32[]{:S(2)}, u32[]{:S(2)}) %all-to-all-start) | async-done | bytes 4194336 | tf_op jit(solution)/shard_map/all_to_all | solution.py:32
  72.9 2.7 %copy.50 = bf16[2,4096,256]{2,1,0:T(8,128)(2,1)S(1)} copy(bf16[2,4096,256]{2,0,1:T(2,128)(2,1)} %all-to-all-done) | data formatting | bytes 8388608 | tf_op jit(solution)/shard_map/all_to_all | solution.py:32
  75.6 2.3 %copy.51 = bf16[4,2,1024,256]{3,2,1,0:T(8,128)(2,1)} copy(bf16[4,2,1024,256]{3,2,0,1:T(8,128)(2,1)S(1)} %bitcast.36) | data formatting | bytes 8388608 | tf_op jit(solution)/shard_map/all_to_all | solution.py:32
  77.9 6.4 %copy.52 = bf16[1024,8,256]{0,2,1:T(8,128)(2,1)} copy(bf16[1024,8,256]{2,0,1:T(8,128)(2,1)} %bitcast.37) | data formatting | bytes 8388608 | tf_op jit(solution)/shard_map/transpose | solution.py:34
  84.4 5.9 %convolution_convert_fusion = bf16[512,2048]{1,0:T(8,128)(2,1)} fusion(bf16[1024,2048]{0,1:T(8,128)(2,1)} %bitcast.34, s32[512]{0:T(512)S(1)} %sub.38), kind=kOutput, calls=%fused_computation | convolution fusion | flops 2149056512 | bytes 6293504 | tf_op jit(solution)/shard_map/while/body/eval_jaxpr/dot_general | solution.py:19
  90.3 4.8 %all-to-all-start.2 = ((bf16[32,16,2048]{2,1,0:T(8,128)(2,1)}), bf16[32,16,2048]{2,1,0:T(8,128)(2,1)S(1)}, u32[]{:S(2)}, u32[]{:S(2)}) async-start(bf16[32,16,2048]{2,1,0:T(8,128)(2,1)} %bitcast.42), calls=%async_computation.2 | async-start | bytes 4194304 | tf_op jit(solution)/shard_map/all_to_all | solution.py:55
  95.1 0.0 copy-done
  95.1 5.6 %fusion.11 = f32[256,2048]{1,0:T(8,128)S(1)} fusion(bf16[256,2560]{1,0:T(8,128)(2,1)S(1)} %copy-done, bf16[2560,2048]{1,0:T(8,128)(2,1)} %param.8), kind=kOutput, calls=%fused_computation.33 | convolution fusion | flops 2684354560 | bytes 13893632 | tf_op jit(solution)/shard_map/dot_general | solution.py:62
  100.7 0.0 copy-start.1
  100.7 0.9 copy.61
  101.6 0.5 copy-done.1
  102.1 0.3 multiply_reduce_fusion
  102.4 0.1 copy.53
  102.5 6.4 %copy.58 = bf16[1,1,1024,2048]{3,2,1,0:T(8,128)(2,1)} copy(bf16[1,1,1024,2048]{2,3,1,0:T(8,128)(2,1)} %bitcast.35) | data formatting | bytes 8388608
  108.9 36.2 %all-to-all-done.2 = bf16[32,16,2048]{2,1,0:T(8,128)(2,1)S(1)} async-done(((bf16[32,16,2048]{2,1,0:T(8,128)(2,1)}), bf16[32,16,2048]{2,1,0:T(8,128)(2,1)S(1)}, u32[]{:S(2)}, u32[]{:S(2)}) %all-to-all-start.2) | async-done | bytes 2097184 | tf_op jit(solution)/shard_map/all_to_all | solution.py:55
  145.1 0.0 copy-start.2
  145.1 2.5 %copy.57 = bf16[512,2048]{0,1:T(8,128)(2,1)} copy(bf16[512,2048]{1,0:T(8,128)(2,1)S(1)} %bitcast.38) | data formatting | bytes 4194304 | tf_op jit(solution)/shard_map/reshape | solution.py:59
  147.6 0.0 copy-done.2
  147.6 3.0 %fusion.3 = bf16[256,8,256]{2,0,1:T(8,128)(2,1)S(1)} fusion(f32[32,8,8,256]{3,2,1,0:T(8,128)} %bitcast.41, bf16[8,256,512]{2,1,0:T(8,128)(2,1)} %bitcast.43, f32[256]{0:T(256)S(1)} %copy-done.2, f32[256,8]{0,1:T(8,128)S(1)} %add_sqrt_fusion, s32[256]{0:T(256)S(1)} %multiply_add_fusion), kind=kOutput, calls=%fused_computation.7 | convolution fusion | flops 540409856 | bytes 5253120 | tf_op jit(solution)/shard_map/dot_general | solution.py:57
  150.6 1.6 %copy.59 = bf16[256,8,256]{2,1,0:T(8,128)(2,1)} copy(bf16[256,8,256]{2,0,1:T(8,128)(2,1)S(1)} %fusion.3) | data formatting | bytes 2097152
  (4 shorter events, 0.1 us)
Async XLA Ops:
  0.6 94.4 %copy-start = (bf16[256,2560]{1,0:T(8,128)(2,1)S(1)}, bf16[256,2560]{1,0:T(8,128)(2,1)}, u32[]{:S(2)}) copy-start(bf16[256,2560]{1,0:T(8,128)(2,1)} %param.7) | copy-start | bytes 3932164
  2.5 17.4 %all-to-all-start.1 = ((s32[32,1,16]{2,1,0:T(1,128)}), s32[32,1,16]{2,1,0:T(1,128)S(1)}, u32[]{:S(2)}, u32[]{:S(2)}) async-start(s32[32,1,16]{2,1,0:T(1,128)} %bitcast.6), calls=%async_computation.1 | async-start | bytes 32768 | tf_op jit(solution)/shard_map/all_to_all | solution.py:50
  19.9 53.0 %all-to-all-start = ((bf16[2,4096,256]{2,0,1:T(2,128)(2,1)}), bf16[2,4096,256]{2,0,1:T(2,128)(2,1)}, u32[]{:S(2)}, u32[]{:S(2)}) async-start(bf16[2,4096,256]{2,0,1:T(2,128)(2,1)} %copy.49), calls=%async_computation | async-start | bytes 8388608 | tf_op jit(solution)/shard_map/all_to_all | solution.py:32
  90.3 54.8 %all-to-all-start.2 = ((bf16[32,16,2048]{2,1,0:T(8,128)(2,1)}), bf16[32,16,2048]{2,1,0:T(8,128)(2,1)S(1)}, u32[]{:S(2)}, u32[]{:S(2)}) async-start(bf16[32,16,2048]{2,1,0:T(8,128)(2,1)} %bitcast.42), calls=%async_computation.2 | async-start | bytes 4194304 | tf_op jit(solution)/shard_map/all_to_all | solution.py:55
  100.7 1.4 copy-start.1
  145.1 2.5 %copy-start.2 = (f32[256]{0:T(256)S(1)}, f32[256]{0:T(256)}, u32[]{:S(2)}) copy-start(f32[256]{0:T(256)} %param.9) | copy-start | bytes 3076
where the time goes:
time: 153 us; the launch traced here: 152 us
  waiting for transfers between devices  84.1 us (55%)
  local copies, waits for them, and re-layouts  34.3 us (22%)
  starting transfers between devices  16.9 us (11%)
  matrix products  14.5 us (9%)
  other arithmetic  1.55 us (1%)
    all_to_all x1, waiting for transfers between devices, on_device(): lax.all_to_all(table, 'grp', split_axis=1, concat_axis=0, tiled=True)  48 us
    all_to_all x1, waiting for transfers between devices, on_device(): lax.all_to_all(found, ('grp', 'dev'), split_axis=0, concat_axis=0, tiled=...  36.2 us
    unnamed x10, local copies, waits for them, and re-layouts  19.5 us
    all_to_all x1, starting transfers between devices, on_device(): lax.all_to_all(outgoing.reshape(peers, capacity), ('grp', 'dev'), split_a...  7.33 us
    transpose x1, local copies, waits for them, and re-layouts, on_device(): jnp.transpose(moved, (1, 0, 2)).reshape(row_count, layers * width)  6.44 us
    dot_general x1, matrix products, one_block(): jnp.dot(onehot, local_rows, preferred_element_type=jnp.float32)  5.91 us
    dot_general x1, matrix products, on_device(): jnp.dot(hidden, w_proj, preferred_element_type=jnp.float32)  5.61 us
    all_to_all x2, local copies, waits for them, and re-layouts, on_device(): lax.all_to_all(table, 'grp', split_axis=1, concat_axis=0, tiled=True)  5.05 us
  transfers between devices with their start and end apart: 3, of which 2 were waited for; matrix products, arithmetic and copies ran while one was open for 15% of the time, Pallas kernels for 0%

commit v1 on v0

v1 whole, which is shorter than its diff:
```python
import functools
import math

import jax
import jax.numpy as jnp
from jax import lax
from jax.experimental import pallas as pl
from jax.experimental.pallas import tpu as pltpu
from jax.sharding import PartitionSpec as P

MESH = pl.DeviceIdType.MESH
LANES = 128


def column(row):
    return jnp.transpose(jnp.broadcast_to(row.astype(jnp.float32), (LANES, LANES)))


def exchange(n_grp, n_dev, cap,
             ids_ref, want_ref, hidden_ref, gain_ref, table_ref, w_ref,
             served_ref, out_ref,
             tbl, wbuf, ids_buf, want_buf, cols, send, recv, esend, erecv, normed,
             ids_ss, ids_rs, want_ss, want_rs, tab_ss, tab_rs, z_ss, z_rs, e_ss, e_rs,
             tbl_sem, w_sem, own_sem):
    g = lax.axis_index("grp")
    d = lax.axis_index("dev")
    layer_share, vocab_share, width = table_ref.shape
    rows = vocab_share // n_grp
    tok = hidden_ref.shape[0]
    layers = layer_share * n_grp
    wide = layer_share * width
    slots = n_grp * cap
    all_slots = n_dev * slots

    def grp_at(i):
        return lax.rem(g + i, n_grp)

    def dev_at(j):
        return lax.rem(d + j, n_dev)

    load_table = pltpu.make_async_copy(table_ref, tbl, tbl_sem)
    load_table.start()
    load_w = pltpu.make_async_copy(w_ref, wbuf, w_sem)
    load_w.start()

    barrier = pltpu.get_barrier_semaphore()
    for i in range(n_grp):
        def greet(j, carry, i=i):
            pl.semaphore_signal(
                barrier, inc=1, device_id={"grp": grp_at(i), "dev": dev_at(j)}, device_id_type=MESH
            )
            return carry
        lax.fori_loop(1 if i == 0 else 0, n_dev, greet, 0)
    pl.semaphore_wait(barrier, n_grp * n_dev - 1)

    def ids_copy(i, j):
        return pltpu.make_async_remote_copy(
            src_ref=ids_ref.at[dev_at(j)], dst_ref=ids_buf.at[g, d],
            send_sem=ids_ss.at[i, j], recv_sem=ids_rs.at[i, j],
            device_id={"grp": grp_at(i), "dev": dev_at(j)}, device_id_type=MESH,
        )

    def want_copy(i):
        return pltpu.make_async_remote_copy(
            src_ref=want_ref, dst_ref=want_buf.at[g],
            send_sem=want_ss.at[i], recv_sem=want_rs.at[i],
            device_id={"grp": grp_at(i), "dev": d}, device_id_type=MESH,
        )

    order = list(range(n_grp - 1, 0, -1)) + [0]
    for i in [(n_grp - o) % n_grp for o in order]:
        def start_ids(j, carry, i=i):
            ids_copy(i, j).start()
            return carry
        lax.fori_loop(1 if i == 0 else 0, n_dev, start_ids, 0)
    for i in range(1, n_grp):
        want_copy(i).start()

    def tab_copy(i, l):
        gp = grp_at(i)
        return pltpu.make_async_remote_copy(
            src_ref=table_ref.at[l, pl.ds(pl.multiple_of(gp * rows, rows), rows), :],
            dst_ref=served_ref.at[:, pl.ds(pl.multiple_of((g * layer_share + l) * width, width), width)],
            send_sem=tab_ss.at[i, l], recv_sem=tab_rs.at[i, l],
            device_id={"grp": gp, "dev": d}, device_id_type=MESH,
        )

    for l in range(layer_share):
        for i in range(1, n_grp):
            tab_copy(i, l).start()

    def own_copy(l):
        return pltpu.make_async_copy(
            tbl.at[l, pl.ds(pl.multiple_of(g * rows, rows), rows), :],
            served_ref.at[:, pl.ds(pl.multiple_of((g * layer_share + l) * width, width), width)],
            own_sem.at[l],
        )

    load_table.wait()
    for l in range(layer_share):
        own_copy(l).start()

    ids_buf[g, d] = ids_ref[d]
    want_buf[g] = want_ref[...]

    def z_copy(o, j):
        dp = dev_at(j)
        gp = grp_at(o)
        return pltpu.make_async_remote_copy(
            src_ref=send.at[o, dp],
            dst_ref=recv.at[gp, pl.ds(pl.multiple_of(d * slots, slots), slots), :],
            send_sem=z_ss.at[o, j], recv_sem=z_rs.at[o, j],
            device_id={"grp": g, "dev": dp}, device_id_type=MESH,
        )

    for o in order:
        gp = grp_at(o)
        back = (n_grp - o) % n_grp

        def take_ids(j, carry, back=back):
            ids_copy(back, j).wait_recv()
            return carry
        lax.fori_loop(1 if back == 0 else 0, n_dev, take_ids, 0)

        def turn(a, carry, gp=gp):
            cols[a] = column(ids_buf[gp, a])
            return carry
        lax.fori_loop(0, n_dev, turn, 0)

        def block(b, carry, o=o):
            at = pl.multiple_of(b * cap, cap)
            wanted = cols[:, pl.ds(at, cap), :].reshape(n_dev * cap, LANES)
            lane = lax.broadcasted_iota(jnp.int32, (n_dev * cap, LANES), 1)
            lane = (lane + (d * n_grp + b) * rows).astype(jnp.float32)
            wanted = wanted - lane
            hit = jnp.concatenate(
                [(wanted == float(c * LANES)).astype(jnp.float32) for c in range(rows // LANES)], axis=1
            ).astype(jnp.bfloat16)
            for l in range(layer_share):
                found = jnp.dot(
                    hit, tbl[l, pl.ds(pl.multiple_of(b * rows, rows), rows), :],
                    preferred_element_type=jnp.float32,
                ).astype(jnp.bfloat16)
                send[o, :, pl.ds(at, cap), l * width:(l + 1) * width] = found.reshape(n_dev, cap, width)
            return carry
        lax.fori_loop(0, n_grp, block, 0)

        def start_z(j, carry, o=o):
            z_copy(o, j).start()
            return carry
        lax.fori_loop(1, n_dev, start_z, 0)
        recv[gp, pl.ds(pl.multiple_of(d * slots, slots), slots), :] = send[o, d]

    load_w.wait()

    def project(l, carry):
        at = pl.multiple_of(l * width, width)
        proj = jnp.dot(hidden_ref[...], wbuf[:, pl.ds(at, width)], preferred_element_type=jnp.float32)
        mean_sq = jnp.mean(proj * proj, axis=-1, keepdims=True)
        normed[l] = proj / jnp.sqrt(mean_sq + 1e-06) * gain_ref[...]
        return carry
    lax.fori_loop(0, layers, project, 0)

    def e_copy(o):
        return pltpu.make_async_remote_copy(
            src_ref=esend.at[o], dst_ref=erecv.at[g],
            send_sem=e_ss.at[o], recv_sem=e_rs.at[o],
            device_id={"grp": grp_at(o), "dev": d}, device_id_type=MESH,
        )

    for o in order:
        gp = grp_at(o)
        if o:
            want_copy(n_grp - o).wait_recv()

        def take_rows(j, carry, o=o):
            z_copy(o, j).wait_recv()
            return carry
        lax.fori_loop(1, n_dev, take_rows, 0)

        for t in range(tok // LANES):
            mine = column(want_buf[gp, t:t + 1, :])
            lane = lax.broadcasted_iota(jnp.int32, (LANES, LANES), 1).astype(jnp.float32)
            mine = mine - lane
            picker = jnp.concatenate(
                [(mine == float(c * LANES)).astype(jnp.float32) for c in range(all_slots // LANES)], axis=1
            ).astype(jnp.bfloat16)
            picked = jnp.dot(picker, recv[gp], preferred_element_type=jnp.float32).astype(jnp.bfloat16)
            if o:
                esend[o, t * LANES:(t + 1) * LANES, :] = picked
            else:
                erecv[g, t * LANES:(t + 1) * LANES, :] = picked
        if o:
            e_copy(o).start()

    for o in range(1, n_grp):
        e_copy(o).wait_recv()

    for l in range(layers):
        at = (l % layer_share) * width
        emb = erecv[l // layer_share, :, at:at + width].astype(jnp.float32)
        mixed = (normed[l] + math.sqrt(width) * emb) / math.sqrt(2.0)
        out_ref[:, l * width:(l + 1) * width] = mixed.astype(jnp.bfloat16)

    for l in range(layer_share):
        own_copy(l).wait()
        for i in range(1, n_grp):
            tab_copy(i, l).wait()
    for i in range(n_grp):
        def end_ids(j, carry, i=i):
            ids_copy(i, j).wait_send()
            return carry
        lax.fori_loop(1 if i == 0 else 0, n_dev, end_ids, 0)

        def end_z(j, carry, i=i):
            z_copy(i, j).wait_send()
            return carry
        lax.fori_loop(1, n_dev, end_z, 0)
        if i:
            want_copy(i).wait_send()
            e_copy(i).wait_send()


def on_device(table, token_ids, hidden, w_proj, norm_gain):
    n_grp = lax.axis_size("grp")
    n_dev = lax.axis_size("dev")
    layer_share, vocab_share, width = table.shape
    layers = layer_share * n_grp
    tok = token_ids.shape[0]
    rows = vocab_share // n_grp
    blocks = n_grp * n_dev
    cap = -(-max(2, 2 * tok // blocks) // 16) * 16
    slots = n_grp * cap
    assert slots <= LANES and tok % LANES == 0 and rows % LANES == 0
    wide = layer_share * width

    owner = token_ids // rows
    positions = jnp.arange(tok, dtype=jnp.int32)
    same = owner[:, None] == owner[None, :]
    earlier = positions[None, :] < positions[:, None]
    slot = jnp.sum((same & earlier).astype(jnp.int32), axis=1)
    wanted = owner * cap + slot
    hit = (wanted[:, None] == jnp.arange(blocks * cap, dtype=jnp.int32)[None, :]).astype(jnp.int32)
    outgoing = jnp.sum(hit * (token_ids + 1)[:, None], axis=0) - 1
    outgoing = outgoing.reshape(n_dev, 1, slots)
    outgoing = jnp.pad(outgoing, ((0, 0), (0, 0), (0, LANES - slots)), constant_values=-1)

    vmem = pl.BlockSpec(memory_space=pltpu.VMEM)
    anywhere = pl.BlockSpec(memory_space=pl.ANY)
    dma = pltpu.SemaphoreType.DMA
    bf16 = jnp.bfloat16
    served, mixed = pl.pallas_call(
        functools.partial(exchange, n_grp, n_dev, cap),
        out_shape=(
            jax.ShapeDtypeStruct((rows, layers * width), bf16),
            jax.ShapeDtypeStruct((tok, layers * width), bf16),
        ),
        in_specs=[vmem, vmem, vmem, vmem, anywhere, anywhere],
        out_specs=(anywhere, vmem),
        scratch_shapes=[
            pltpu.VMEM(table.shape, bf16),
            pltpu.VMEM(w_proj.shape, bf16),
            pltpu.VMEM((n_grp, n_dev, 1, LANES), jnp.int32),
            pltpu.VMEM((n_grp, tok // LANES, LANES), jnp.int32),
            pltpu.VMEM((n_dev, LANES, LANES), jnp.float32),
            pltpu.VMEM((n_grp, n_dev, slots, wide), bf16),
            pltpu.VMEM((n_grp, n_dev * slots, wide), bf16),
            pltpu.VMEM((n_grp, tok, wide), bf16),
            pltpu.VMEM((n_grp, tok, wide), bf16),
            pltpu.VMEM((layers, tok, width), jnp.float32),
            dma((n_grp, n_dev)), dma((n_grp, n_dev)),
            dma((n_grp,)), dma((n_grp,)),
            dma((n_grp, layer_share)), dma((n_grp, layer_share)),
            dma((n_grp, n_dev)), dma((n_grp, n_dev)),
            dma((n_grp,)), dma((n_grp,)),
            dma, dma, dma((layer_share,)),
        ],
        compiler_params=pltpu.CompilerParams(
            collective_id=0, has_side_effects=True, vmem_limit_bytes=56 * 2**20
        ),
        name="exchange",
    )(outgoing, wanted.reshape(tok // LANES, LANES), hidden, norm_gain.reshape(1, width), table, w_proj)
    return (
        served.reshape(1, 1, rows, layers * width),
        mixed.reshape(tok, layers, width),
    )


def solution(mesh):
    in_specs = (P("grp", "dev", None), P(("grp", "dev")), P(("grp", "dev"), None), P(), P())
    out_specs = (P("dev", "grp", None, None), P(("grp", "dev"), None, None))
    return jax.shard_map(
        on_device, mesh=mesh, in_specs=in_specs, out_specs=out_specs, check_vma=False
    )
```

time: 153 us -> 79.8 us (0.52)
  waiting for transfers between devices: 84.1 us -> 0 us
  Pallas kernels: 0 us -> 69.9 us
  local copies, waits for them, and re-layouts: 34.3 us -> 7.98 us
  starting transfers between devices: 16.9 us -> 0 us
  matrix products: 14.5 us -> 0 us
    all_to_all x3 -> x0, waiting for transfers between devices: 84.1 us -> none  [the longest x1 48 us: on_device(): lax.all_to_all(table, 'grp', split_axis=1, concat_axis=0, tiled=True)]
    pallas_call x0 -> x1, Pallas kernels: none -> 69.9 us  [on_device(): pl.pallas_call(functools.partial(exchange, n_grp, n_dev, cap), out_shape=...]
    all_to_all x3 -> x0, starting transfers between devices: 16.9 us -> none  [the longest x1 7.33 us: on_device(): lax.all_to_all(outgoing.reshape(peers, capacity), ('grp', 'dev'), split_a...]
    dot_general x3 -> x0, matrix products: 14.5 us -> none  [the longest x1 5.91 us: one_block(): jnp.dot(onehot, local_rows, preferred_element_type=jnp.float32)]
    unnamed x10 -> x4, local copies, waits for them, and re-layouts: 19.5 us -> 7.3 us
    transpose x1 -> x0, local copies, waits for them, and re-layouts: 6.44 us -> none  [on_device(): jnp.transpose(moved, (1, 0, 2)).reshape(row_count, layers * width)]
    all_to_all x2 -> x0, local copies, waits for them, and re-layouts: 5.05 us -> none  [on_device(): lax.all_to_all(table, 'grp', split_axis=1, concat_axis=0, tiled=True)]
    reshape x1 -> x0, local copies, waits for them, and re-layouts: 2.5 us -> none  [on_device(): replies.reshape(peers * capacity, layers * width)]
  transfers between devices with their start and end apart: 3 -> 0, of which waited for: 2 -> 0; matrix products, arithmetic and copies ran while one was open for 15% -> 0% of each run, Pallas kernels for 0% -> 0%
where the time goes in v1:
time: 79.8 us; the launch traced here: 79.6 us
  Pallas kernels  69.9 us (88%)
  local copies, waits for them, and re-layouts  7.98 us (10%)
  other arithmetic  1.03 us (1%)
    pallas_call x1, Pallas kernels, on_device(): pl.pallas_call(functools.partial(exchange, n_grp, n_dev, cap), out_shape=...  69.9 us
    unnamed x4, local copies, waits for them, and re-layouts  7.3 us

profile of v1, /device:TPU:0, one launch (start us, length us, event | category | flops | bytes accessed | tf_op | source)
XLA Modules:
  0.0 79.6 jit_solution(2105581949587350781)
XLA Ops:
  0.6 0.7 and_select_fusion
  1.3 0.2 convert_reduce_fusion
  1.5 0.0 copy-start
  1.5 0.1 select_reduce_fusion
  1.7 0.1 sub.14
  1.8 0.6 pad.4.ids_ref
  2.4 0.0 copy-done
  2.4 69.9 %exchange.1 = (bf16[1024,2048]{1,0:T(8,128)(2,1)}, bf16[256,2048]{1,0:T(8,128)(2,1)}) custom-call(s32[8,1,128]{2,1,0:T(1,128)} %pad.4.ids_ref, s32[2,128]{1,0:T(2,128)} %bitcast.8, bf16[256,2560]{1,0:T(8,128)(2,1)} %hidden_ref.1, f32[1,256]{1,0:T(1,128)} %bitcast.9, bf16[2,4096,256]{2,1,0:T(8,128)(2,1)} %table_ref.1, bf16[2560,2048]{1,0:T(8,128)(2,1)} %w_ref.1), custom_call_target="tpu_custom_call" | custom-call | tf_op jit(solution)/shard_map/exchange/pallas_call | solution.py:252
  72.3 2.5 %copy.7 = bf16[32,8,8,256]{3,2,1,0:T(8,128)(2,1)} copy(bf16[32,8,8,256]{3,1,2,0:T(8,128)(2,1)} %bitcast.7) | data formatting | bytes 2097152
  74.8 4.8 %copy.9 = bf16[1,1,1024,2048]{3,2,1,0:T(8,128)(2,1)} copy(bf16[1,1,1024,2048]{3,2,1,0:T(8,128)(2,1)} %bitcast.5) | data formatting | bytes 8388608
  (2 shorter events, 0.0 us)
Async XLA Ops:
  1.5 0.9 %copy-start = (s32[256]{0:T(256)}, s32[256]{0:T(256)S(1)}, u32[]{:S(2)}) copy-start(s32[256]{0:T(256)S(1)} %multiply_add_fusion) | copy-start | bytes 3076

commit v2 on v1

--- a/solution.py
+++ b/solution.py
@@ -10,6 +10,7 @@
 
 MESH = pl.DeviceIdType.MESH
 LANES = 128
+PIECES = 4
 
 
 def column(row):
@@ -19,7 +20,7 @@
 def exchange(n_grp, n_dev, cap,
              ids_ref, want_ref, hidden_ref, gain_ref, table_ref, w_ref,
              served_ref, out_ref,
-             tbl, wbuf, ids_buf, want_buf, cols, send, recv, esend, erecv, normed,
+             tbl, wbuf, ids_buf, want_buf, cols, send, recv, esend, erecv, mix,
              ids_ss, ids_rs, want_ss, want_rs, tab_ss, tab_rs, z_ss, z_rs, e_ss, e_rs,
              tbl_sem, w_sem, own_sem):
     g = lax.axis_index("grp")
@@ -76,29 +77,40 @@
     for i in range(1, n_grp):
         want_copy(i).start()
 
-    def tab_copy(i, l):
+    part = rows // PIECES
+    pieces = [(l, p) for l in range(layer_share) for p in range(PIECES)]
+
+    def tab_copy(i, l, p):
         gp = grp_at(i)
         return pltpu.make_async_remote_copy(
-            src_ref=table_ref.at[l, pl.ds(pl.multiple_of(gp * rows, rows), rows), :],
-            dst_ref=served_ref.at[:, pl.ds(pl.multiple_of((g * layer_share + l) * width, width), width)],
-            send_sem=tab_ss.at[i, l], recv_sem=tab_rs.at[i, l],
+            src_ref=table_ref.at[l, pl.ds(pl.multiple_of(gp * rows + p * part, part), part), :],
+            dst_ref=served_ref.at[
+                pl.ds(p * part, part),
+                pl.ds(pl.multiple_of((g * layer_share + l) * width, width), width),
+            ],
+            send_sem=tab_ss.at[i, l, p], recv_sem=tab_rs.at[i, l, p],
             device_id={"grp": gp, "dev": d}, device_id_type=MESH,
         )
 
-    for l in range(layer_share):
-        for i in range(1, n_grp):
-            tab_copy(i, l).start()
+    def start_pieces(first, last):
+        for l, p in pieces[first:last]:
+            for i in range(1, n_grp):
+                tab_copy(i, l, p).start()
+
+    ahead = len(pieces) * 3 // 4
+    middle = len(pieces) * 7 // 8
+    start_pieces(0, ahead)
 
     def own_copy(l):
         return pltpu.make_async_copy(
-            tbl.at[l, pl.ds(pl.multiple_of(g * rows, rows), rows), :],
+            table_ref.at[l, pl.ds(pl.multiple_of(g * rows, rows), rows), :],
             served_ref.at[:, pl.ds(pl.multiple_of((g * layer_share + l) * width, width), width)],
             own_sem.at[l],
         )
 
-    load_table.wait()
     for l in range(layer_share):
         own_copy(l).start()
+    load_table.wait()
 
     ids_buf[g, d] = ids_ref[d]
     want_buf[g] = want_ref[...]
@@ -153,13 +165,13 @@
 
     load_w.wait()
 
-    def project(l, carry):
-        at = pl.multiple_of(l * width, width)
-        proj = jnp.dot(hidden_ref[...], wbuf[:, pl.ds(at, width)], preferred_element_type=jnp.float32)
+    def project(l):
+        proj = jnp.dot(hidden_ref[...], wbuf[:, l * width:(l + 1) * width], preferred_element_type=jnp.float32)
         mean_sq = jnp.mean(proj * proj, axis=-1, keepdims=True)
-        normed[l] = proj / jnp.sqrt(mean_sq + 1e-06) * gain_ref[...]
-        return carry
-    lax.fori_loop(0, layers, project, 0)
+        return proj / jnp.sqrt(mean_sq + 1e-06) * gain_ref[...]
+
+    for l in range(layers):
+        mix[:, l, :] = project(l)
 
     def e_copy(o):
         return pltpu.make_async_remote_copy(
@@ -192,6 +204,10 @@
                 erecv[g, t * LANES:(t + 1) * LANES, :] = picked
         if o:
             e_copy(o).start()
+        if o == order[-3 if n_grp > 2 else -2]:
+            start_pieces(ahead, middle)
+        if o == order[-2]:
+            start_pieces(middle, len(pieces))
 
     for o in range(1, n_grp):
         e_copy(o).wait_recv()
@@ -199,13 +215,14 @@
     for l in range(layers):
         at = (l % layer_share) * width
         emb = erecv[l // layer_share, :, at:at + width].astype(jnp.float32)
-        mixed = (normed[l] + math.sqrt(width) * emb) / math.sqrt(2.0)
-        out_ref[:, l * width:(l + 1) * width] = mixed.astype(jnp.bfloat16)
+        mix[:, l, :] = (mix[:, l, :] + math.sqrt(width) * emb) / math.sqrt(2.0)
+    out_ref[...] = mix[...].astype(jnp.bfloat16)
 
     for l in range(layer_share):
         own_copy(l).wait()
+    for l, p in pieces:
         for i in range(1, n_grp):
-            tab_copy(i, l).wait()
+            tab_copy(i, l, p).wait()
     for i in range(n_grp):
         def end_ids(j, carry, i=i):
             ids_copy(i, j).wait_send()
@@ -252,11 +269,11 @@
     served, mixed = pl.pallas_call(
         functools.partial(exchange, n_grp, n_dev, cap),
         out_shape=(
-            jax.ShapeDtypeStruct((rows, layers * width), bf16),
-            jax.ShapeDtypeStruct((tok, layers * width), bf16),
+            pltpu.VMEM((rows, layers * width), bf16),
+            pltpu.VMEM((tok, layers, width), bf16),
         ),
         in_specs=[vmem, vmem, vmem, vmem, anywhere, anywhere],
-        out_specs=(anywhere, vmem),
+        out_specs=(vmem, vmem),
         scratch_shapes=[
             pltpu.VMEM(table.shape, bf16),
             pltpu.VMEM(w_proj.shape, bf16),
@@ -267,23 +284,20 @@
             pltpu.VMEM((n_grp, n_dev * slots, wide), bf16),
             pltpu.VMEM((n_grp, tok, wide), bf16),
             pltpu.VMEM((n_grp, tok, wide), bf16),
-            pltpu.VMEM((layers, tok, width), jnp.float32),
+            pltpu.VMEM((tok, layers, width), jnp.float32),
             dma((n_grp, n_dev)), dma((n_grp, n_dev)),
             dma((n_grp,)), dma((n_grp,)),
-            dma((n_grp, layer_share)), dma((n_grp, layer_share)),
+            dma((n_grp, layer_share, PIECES)), dma((n_grp, layer_share, PIECES)),
             dma((n_grp, n_dev)), dma((n_grp, n_dev)),
             dma((n_grp,)), dma((n_grp,)),
             dma, dma, dma((layer_share,)),
         ],
         compiler_params=pltpu.CompilerParams(
-            collective_id=0, has_side_effects=True, vmem_limit_bytes=56 * 2**20
+            collective_id=0, has_side_effects=True, vmem_limit_bytes=44 * 2**20
         ),
         name="exchange",
     )(outgoing, wanted.reshape(tok // LANES, LANES), hidden, norm_gain.reshape(1, width), table, w_proj)
-    return (
-        served.reshape(1, 1, rows, layers * width),
-        mixed.reshape(tok, layers, width),
-    )
+    return (served.reshape(1, 1, rows, layers * width), mixed)
 
 
 def solution(mesh):

time: 79.8 us -> 80.2 us (level)
  the two profiles are of different devices: /device:TPU:0 before, /device:TPU:9 now
where the time goes in v2:
time: 80.2 us; the launch traced here: 80 us
  Pallas kernels  73.3 us (91%)
  local copies, waits for them, and re-layouts  5.07 us (6%)
  other arithmetic  1.03 us (1%)
    pallas_call x1, Pallas kernels, on_device(): pl.pallas_call(functools.partial(exchange, n_grp, n_dev, cap), out_shape=...  73.3 us
    unnamed x6, local copies, waits for them, and re-layouts  4.98 us

profile of v2, /device:TPU:9, one launch (start us, length us, event | category | flops | bytes accessed | tf_op | source)
XLA Modules:
  0.0 80.0 jit_solution(4949728212596079860)
XLA Ops:
  0.6 0.7 and_select_fusion
  1.3 0.2 convert_reduce_fusion
  1.5 0.2 select_reduce_fusion
  1.7 0.1 sub.14
  1.8 0.0 copy-start
  1.8 1.3 %copy-done = bf16[256,2560]{1,0:T(8,128)(2,1)S(1)} copy-done((bf16[256,2560]{1,0:T(8,128)(2,1)S(1)}, bf16[256,2560]{1,0:T(8,128)(2,1)}, u32[]{:S(2)}) %copy-start) | copy-done | bytes 1310744
  3.1 0.0 copy-start.1
  3.1 0.7 copy-done.1
  3.8 73.3 %exchange.1 = (bf16[1024,2048]{1,0:T(8,128)(2,1)S(1)}, bf16[256,8,256]{2,1,0:T(8,128)(2,1)S(1)}) custom-call(s32[8,1,128]{2,1,0:T(1,128)S(1)} %pad.4.ids_ref, s32[2,128]{1,0:T(2,128)S(1)} %bitcast.4, bf16[256,2560]{1,0:T(8,128)(2,1)S(1)} %copy-done, f32[1,256]{1,0:T(1,128)S(1)} %bitcast.5, bf16[2,4096,256]{2,1,0:T(8,128)(2,1)} %table_ref.1, ...), custom_call_target="tpu_custom_call" | custom-call | tf_op jit(solution)/shard_map/exchange/pallas_call | solution.py:269
  77.1 2.0 %copy.9 = bf16[1,1,1024,2048]{3,2,1,0:T(8,128)(2,1)} copy(bf16[1,1,1024,2048]{3,2,1,0:T(8,128)(2,1)S(1)} %bitcast.3) | data formatting | bytes 8388608
  79.1 1.0 %copy.10 = bf16[256,8,256]{2,1,0:T(8,128)(2,1)} copy(bf16[256,8,256]{2,1,0:T(8,128)(2,1)S(1)} %get-tuple-element.9) | data formatting | bytes 2097152
  (3 shorter events, 0.0 us)
Async XLA Ops:
  1.8 1.3 %copy-start = (bf16[256,2560]{1,0:T(8,128)(2,1)S(1)}, bf16[256,2560]{1,0:T(8,128)(2,1)}, u32[]{:S(2)}) copy-start(bf16[256,2560]{1,0:T(8,128)(2,1)} %hidden_ref.1) | copy-start | bytes 3932164
  3.1 0.7 copy-start.1

commit v3 on v2

--- a/solution.py
+++ b/solution.py
@@ -18,11 +18,11 @@
 
 
 def exchange(n_grp, n_dev, cap,
-             ids_ref, want_ref, hidden_ref, gain_ref, table_ref, w_ref,
+             ids_ref, want_ref, hidden_hbm, gain_hbm, table_ref, w_ref,
              served_ref, out_ref,
-             tbl, wbuf, ids_buf, want_buf, cols, send, recv, esend, erecv, mix,
+             hidden_ref, gain_ref, tbl, wbuf, ids_buf, want_buf, cols, send, recv, esend, erecv, mix,
              ids_ss, ids_rs, want_ss, want_rs, tab_ss, tab_rs, z_ss, z_rs, e_ss, e_rs,
-             tbl_sem, w_sem, own_sem):
+             tbl_sem, w_sem, hidden_sem, gain_sem, own_sem):
     g = lax.axis_index("grp")
     d = lax.axis_index("dev")
     layer_share, vocab_share, width = table_ref.shape
@@ -43,6 +43,10 @@
     load_table.start()
     load_w = pltpu.make_async_copy(w_ref, wbuf, w_sem)
     load_w.start()
+    load_hidden = pltpu.make_async_copy(hidden_hbm, hidden_ref, hidden_sem)
+    load_hidden.start()
+    load_gain = pltpu.make_async_copy(gain_hbm, gain_ref, gain_sem)
+    load_gain.start()
 
     barrier = pltpu.get_barrier_semaphore()
     for i in range(n_grp):
@@ -97,8 +101,7 @@
             for i in range(1, n_grp):
                 tab_copy(i, l, p).start()
 
-    ahead = len(pieces) * 3 // 4
-    middle = len(pieces) * 7 // 8
+    ahead = len(pieces) * 7 // 8
     start_pieces(0, ahead)
 
     def own_copy(l):
@@ -164,6 +167,8 @@
         recv[gp, pl.ds(pl.multiple_of(d * slots, slots), slots), :] = send[o, d]
 
     load_w.wait()
+    load_hidden.wait()
+    load_gain.wait()
 
     def project(l):
         proj = jnp.dot(hidden_ref[...], wbuf[:, l * width:(l + 1) * width], preferred_element_type=jnp.float32)
@@ -204,10 +209,8 @@
                 erecv[g, t * LANES:(t + 1) * LANES, :] = picked
         if o:
             e_copy(o).start()
-        if o == order[-3 if n_grp > 2 else -2]:
-            start_pieces(ahead, middle)
         if o == order[-2]:
-            start_pieces(middle, len(pieces))
+            start_pieces(ahead, len(pieces))
 
     for o in range(1, n_grp):
         e_copy(o).wait_recv()
@@ -263,7 +266,7 @@
     outgoing = jnp.pad(outgoing, ((0, 0), (0, 0), (0, LANES - slots)), constant_values=-1)
 
     vmem = pl.BlockSpec(memory_space=pltpu.VMEM)
-    anywhere = pl.BlockSpec(memory_space=pl.ANY)
+    hbm = pl.BlockSpec(memory_space=pltpu.HBM)
     dma = pltpu.SemaphoreType.DMA
     bf16 = jnp.bfloat16
     served, mixed = pl.pallas_call(
@@ -272,9 +275,11 @@
             pltpu.VMEM((rows, layers * width), bf16),
             pltpu.VMEM((tok, layers, width), bf16),
         ),
-        in_specs=[vmem, vmem, vmem, vmem, anywhere, anywhere],
+        in_specs=[vmem, vmem, hbm, hbm, hbm, hbm],
         out_specs=(vmem, vmem),
         scratch_shapes=[
+            pltpu.VMEM(hidden.shape, bf16),
+            pltpu.VMEM((1, width), jnp.float32),
             pltpu.VMEM(table.shape, bf16),
             pltpu.VMEM(w_proj.shape, bf16),
             pltpu.VMEM((n_grp, n_dev, 1, LANES), jnp.int32),
@@ -290,7 +295,7 @@
             dma((n_grp, layer_share, PIECES)), dma((n_grp, layer_share, PIECES)),
             dma((n_grp, n_dev)), dma((n_grp, n_dev)),
             dma((n_grp,)), dma((n_grp,)),
-            dma, dma, dma((layer_share,)),
+            dma, dma, dma, dma, dma((layer_share,)),
         ],
         compiler_params=pltpu.CompilerParams(
             collective_id=0, has_side_effects=True, vmem_limit_bytes=44 * 2**20

time: 80.2 us -> 75.2 us (0.938)
  the two profiles are of different devices: /device:TPU:9 before, /device:TPU:0 now
where the time goes in v3:
time: 75.2 us; the launch traced here: 75 us
  Pallas kernels  68.2 us (91%)
  local copies, waits for them, and re-layouts  5.07 us (7%)
  other arithmetic  1.03 us (1%)
    pallas_call x1, Pallas kernels, on_device(): pl.pallas_call(functools.partial(exchange, n_grp, n_dev, cap), out_shape=...  68.2 us
    unnamed x6, local copies, waits for them, and re-layouts  4.98 us

profile of v3, /device:TPU:0, one launch (start us, length us, event | category | flops | bytes accessed | tf_op | source)
XLA Modules:
  0.0 75.0 jit_solution(11268477599767418397)
XLA Ops:
  0.6 0.7 and_select_fusion
  1.3 0.2 convert_reduce_fusion
  1.5 0.2 select_reduce_fusion
  1.7 0.1 sub.14
  1.8 0.0 copy-start
  1.8 1.3 %copy-done = bf16[256,2560]{1,0:T(8,128)(2,1)S(1)} copy-done((bf16[256,2560]{1,0:T(8,128)(2,1)S(1)}, bf16[256,2560]{1,0:T(8,128)(2,1)}, u32[]{:S(2)}) %copy-start) | copy-done | bytes 1310744
  3.1 0.0 copy-start.1
  3.1 0.7 copy-done.1
  3.8 68.2 %exchange.1 = (bf16[1024,2048]{1,0:T(8,128)(2,1)S(1)}, bf16[256,8,256]{2,1,0:T(8,128)(2,1)S(1)}) custom-call(s32[8,1,128]{2,1,0:T(1,128)S(1)} %pad.4.ids_ref, s32[2,128]{1,0:T(2,128)S(1)} %bitcast.4, bf16[256,2560]{1,0:T(8,128)(2,1)S(1)} %copy-done, f32[1,256]{1,0:T(1,128)S(1)} %bitcast.5, bf16[2,4096,256]{2,1,0:T(8,128)(2,1)} %table_ref.1, ...), custom_call_target="tpu_custom_call" | custom-call | tf_op jit(solution)/shard_map/exchange/pallas_call | solution.py:272
  72.0 2.0 %copy.9 = bf16[1,1,1024,2048]{3,2,1,0:T(8,128)(2,1)} copy(bf16[1,1,1024,2048]{3,2,1,0:T(8,128)(2,1)S(1)} %bitcast.3) | data formatting | bytes 8388608
  74.0 1.0 %copy.10 = bf16[256,8,256]{2,1,0:T(8,128)(2,1)} copy(bf16[256,8,256]{2,1,0:T(8,128)(2,1)S(1)} %get-tuple-element.9) | data formatting | bytes 2097152
  (3 shorter events, 0.0 us)
Async XLA Ops:
  1.8 1.3 %copy-start = (bf16[256,2560]{1,0:T(8,128)(2,1)S(1)}, bf16[256,2560]{1,0:T(8,128)(2,1)}, u32[]{:S(2)}) copy-start(bf16[256,2560]{1,0:T(8,128)(2,1)} %hidden_hbm.1) | copy-start | bytes 3932164
  3.1 0.7 copy-start.1
